TPU v7x, 32 devices: a whole 2x2x4 slice. The times are simulated.
32 devices in a mesh: ctx: 8 (over z, y), dp: 4 (over x, core).
Axes of the slice: x: 2, y: 2, z: 4, core: 2. Of those that a mesh axis runs over, the one named last changes fastest.
Arguments:
- tokens: bfloat16 [8, 512, 4096], P('dp', 'ctx'), may hold values from -6 to 6
- queries: bfloat16 [8, 512, 2048], P('dp', 'ctx'), may hold values from -160 to 160
- d_attended: bfloat16 [8, 512, 2048], P('dp', 'ctx'), may hold values from -6 to 6
- span_order: int32 [16], replicated, may hold values from 0 to 15, each once
- norm_gain: float32 [4096], replicated, may hold values from 0.1 to 1.9
- key_weight: bfloat16 [4096, 512], replicated, may hold values from -0.09375 to 0.09375
- value_weight: bfloat16 [4096, 512], replicated, may hold values from -0.09375 to 0.09375
Outputs:
- attended: bfloat16 [8, 512, 2048], P('dp', 'ctx')
- grad_queries: bfloat16 [8, 512, 2048], P('dp', 'ctx')
- grad_tokens: bfloat16 [8, 512, 4096], P('dp', 'ctx')
- grad_key_weight: float32 [4096, 512], P(('ctx', 'dp'))
- grad_value_weight: float32 [4096, 512], P(('ctx', 'dp'))
- grad_gain: float32 [4096], P(('ctx', 'dp'))
All inputs are finite; a program needn't handle non-finite values.
Results may differ from a plain program's by a relative error of at most 0.025.
The roundings to bfloat16 on the way count: a program that leaves them out, or rounds other values in their place, can miss the bound.
Values may be sent and summed in bfloat16 or wider, within the bound.
A program may use at most 192 MiB of HBM per device.

v0:
```python
import jax
import jax.numpy as jnp
from jax import lax
from jax.sharding import PartitionSpec as P

KV_HEADS = 4
HEAD_DIM = 128
ROPE_BASE = 500000.0
EPSILON = 1e-05


def positions(span_order, span_len):
    offsets = jnp.arange(span_len, dtype=jnp.int32)
    return (span_order[:, None] * span_len + offsets[None, :]).reshape(-1)


def rotation(token_pos, head_size):
    half_dim = head_size // 2
    frequency = ROPE_BASE ** (-2.0 * jnp.arange(half_dim, dtype=jnp.float32) / head_size)
    angles = token_pos.astype(jnp.float32)[:, None] * frequency[None, :]
    angles = jnp.concatenate([angles, angles], axis=1)
    return (jnp.cos(angles), jnp.sin(angles))


def rotate_half(values):
    half_dim = values.shape[-1] // 2
    return jnp.concatenate([-values[..., half_dim:], values[..., :half_dim]], axis=-1)


def rotate_back(values):
    half_dim = values.shape[-1] // 2
    return jnp.concatenate([values[..., half_dim:], -values[..., :half_dim]], axis=-1)


def normalize(tokens, norm_gain):
    widened = tokens.astype(jnp.float32)
    rms_scale = lax.rsqrt(jnp.mean(widened * widened, axis=-1, keepdims=True) + EPSILON)
    return ((widened * rms_scale * norm_gain).astype(jnp.bfloat16), rms_scale)


def project_keys(normed, key_weight, value_weight, cosine, sine_table, kv_heads, head_size):
    row_count = normed.shape[0]
    key_pre = jnp.dot(normed, key_weight, preferred_element_type=jnp.float32).reshape(
        row_count, kv_heads, head_size
    )
    rotated = key_pre * cosine[:, None, :] + rotate_half(key_pre) * sine_table[:, None, :]
    value_rows = jnp.dot(normed, value_weight, preferred_element_type=jnp.float32)
    return (
        rotated.reshape(row_count, kv_heads * head_size).astype(jnp.bfloat16),
        value_rows.astype(jnp.bfloat16),
    )


def attend_group(query_group, grad_group, key_group, value_group, causal_mask, score_scale):
    scores = (
        jnp.einsum("tgd,sd->gts", query_group, key_group, preferred_element_type=jnp.float32)
        * score_scale
    )
    scores = jnp.where(causal_mask[None], scores, -1e30)
    row_max = jnp.max(scores, axis=-1, keepdims=True)
    exponent = jnp.exp(scores - row_max)
    probability = exponent / jnp.sum(exponent, axis=-1, keepdims=True)
    probability_b = probability.astype(jnp.bfloat16)
    attended = jnp.einsum(
        "gts,sd->tgd", probability_b, value_group, preferred_element_type=jnp.float32
    ).astype(jnp.bfloat16)
    dprob = jnp.einsum("tgd,sd->gts", grad_group, value_group, preferred_element_type=jnp.float32)
    delta = jnp.sum(grad_group.astype(jnp.float32) * attended.astype(jnp.float32), axis=-1)
    dscores = (probability * (dprob - jnp.transpose(delta)[:, :, None])).astype(jnp.bfloat16)
    dquery = (
        jnp.einsum("gts,sd->tgd", dscores, key_group, preferred_element_type=jnp.float32)
        * score_scale
    ).astype(jnp.bfloat16)
    key_term = (
        jnp.einsum("gts,tgd->sd", dscores, query_group, preferred_element_type=jnp.float32)
        * score_scale
    )
    value_term = jnp.einsum(
        "gts,tgd->sd", probability_b, grad_group, preferred_element_type=jnp.float32
    )
    return (attended, dquery, key_term, value_term)


def attend_device(queries, grads, all_keys, all_values, query_pos, key_pos, kv_heads, head_size):
    row_count = queries.shape[0]
    group_size = queries.shape[1] // (kv_heads * head_size)
    group_width = group_size * head_size
    causal_mask = key_pos[None, :] <= query_pos[:, None]
    score_scale = head_size ** (-0.5)
    outputs = []
    for head_group in range(kv_heads):
        query_group = queries[:, head_group * group_width : (head_group + 1) * group_width].reshape(
            row_count, group_size, head_size
        )
        grad_group = grads[:, head_group * group_width : (head_group + 1) * group_width].reshape(
            row_count, group_size, head_size
        )
        key_group = all_keys[:, head_group * head_size : (head_group + 1) * head_size]
        value_group = all_values[:, head_group * head_size : (head_group + 1) * head_size]
        outputs.append(
            attend_group(query_group, grad_group, key_group, value_group, causal_mask, score_scale)
        )
    attended = jnp.concatenate(
        [item[0].reshape(row_count, group_width) for item in outputs], axis=1
    )
    dquery = jnp.concatenate([item[1].reshape(row_count, group_width) for item in outputs], axis=1)
    key_terms = jnp.concatenate([item[2] for item in outputs], axis=1)
    value_terms = jnp.concatenate([item[3] for item in outputs], axis=1)
    return (attended, dquery, key_terms, value_terms)


def finish_backward(
    tokens,
    normed,
    rms_scale,
    key_grad,
    value_grad,
    cosine,
    sine_table,
    norm_gain,
    key_weight,
    value_weight,
    kv_heads,
    head_size,
):
    row_count = tokens.shape[0]
    shaped = key_grad.reshape(row_count, kv_heads, head_size)
    key_pre_grad = (
        (shaped * cosine[:, None, :] + rotate_back(shaped * sine_table[:, None, :]))
        .reshape(row_count, kv_heads * head_size)
        .astype(jnp.bfloat16)
    )
    value_pre_grad = value_grad.astype(jnp.bfloat16)
    weight_key = jnp.dot(normed.T, key_pre_grad, preferred_element_type=jnp.float32)
    weight_value = jnp.dot(normed.T, value_pre_grad, preferred_element_type=jnp.float32)
    normed_grad = jnp.dot(key_pre_grad, key_weight.T, preferred_element_type=jnp.float32) + jnp.dot(
        value_pre_grad, value_weight.T, preferred_element_type=jnp.float32
    )
    widened = tokens.astype(jnp.float32)
    gain_part = jnp.sum(normed_grad * widened * rms_scale, axis=0)
    inner_mean = jnp.mean(normed_grad * norm_gain * widened, axis=-1, keepdims=True)
    grad_rows = (
        rms_scale * norm_gain * normed_grad - widened * rms_scale**3 * inner_mean
    ).astype(jnp.bfloat16)
    return (grad_rows, weight_key, weight_value, gain_part)


def body(tokens, queries, d_attended, span_order, norm_gain, key_weight, value_weight):
    local_seqs = tokens.shape[0]
    row_count = tokens.shape[1]
    model_width = tokens.shape[2]
    kv_width = key_weight.shape[1]
    shard_index = lax.axis_index("ctx")
    token_pos = positions(span_order, row_count // 2)
    query_pos = lax.dynamic_slice_in_dim(token_pos, shard_index * row_count, row_count, 0)
    cosine, sine_table = rotation(query_pos, HEAD_DIM)
    cosine_all = jnp.tile(cosine, (local_seqs, 1))
    sine_all = jnp.tile(sine_table, (local_seqs, 1))
    flat_tokens = tokens.reshape(local_seqs * row_count, model_width)
    normed, rms_scale = normalize(flat_tokens, norm_gain)
    rotated_keys, value_rows = project_keys(
        normed, key_weight, value_weight, cosine_all, sine_all, KV_HEADS, HEAD_DIM
    )
    rotated_keys = rotated_keys.reshape(local_seqs, row_count, kv_width)
    value_rows = value_rows.reshape(local_seqs, row_count, kv_width)
    all_keys, all_values = (
        lax.all_gather(rotated_keys, "ctx", axis=1, tiled=True),
        lax.all_gather(value_rows, "ctx", axis=1, tiled=True),
    )
    attended_list, dquery_list, key_list, value_list = ([], [], [], [])
    for sequence in range(local_seqs):
        attended, dquery, key_terms, value_terms = attend_device(
            queries[sequence],
            d_attended[sequence],
            all_keys[sequence],
            all_values[sequence],
            query_pos,
            token_pos,
            KV_HEADS,
            HEAD_DIM,
        )
        attended_list.append(attended)
        dquery_list.append(dquery)
        key_list.append(key_terms)
        value_list.append(value_terms)
    key_stack = jnp.stack(key_list)
    value_stack = jnp.stack(value_list)
    key_grad, value_grad = (
        lax.psum_scatter(
            key_stack.astype(jnp.bfloat16), "ctx", scatter_dimension=1, tiled=True
        ).astype(jnp.float32),
        lax.psum_scatter(
            value_stack.astype(jnp.bfloat16), "ctx", scatter_dimension=1, tiled=True
        ).astype(jnp.float32),
    )
    key_grad = key_grad.reshape(local_seqs * row_count, kv_width)
    value_grad = value_grad.reshape(local_seqs * row_count, kv_width)
    grad_rows, weight_key, weight_value, gain_part = finish_backward(
        flat_tokens,
        normed,
        rms_scale,
        key_grad,
        value_grad,
        cosine_all,
        sine_all,
        norm_gain,
        key_weight,
        value_weight,
        KV_HEADS,
        HEAD_DIM,
    )
    weight_key, weight_value, gain_part = (
        lax.psum_scatter(
            weight_key.astype(jnp.bfloat16), "ctx", scatter_dimension=0, tiled=True
        ).astype(jnp.float32),
        lax.psum_scatter(
            weight_value.astype(jnp.bfloat16), "ctx", scatter_dimension=0, tiled=True
        ).astype(jnp.float32),
        lax.psum_scatter(
            gain_part.astype(jnp.bfloat16), "ctx", scatter_dimension=0, tiled=True
        ).astype(jnp.float32),
    )
    weight_key, weight_value, gain_part = (
        lax.psum_scatter(
            weight_key.astype(jnp.bfloat16), "dp", scatter_dimension=0, tiled=True
        ).astype(jnp.float32),
        lax.psum_scatter(
            weight_value.astype(jnp.bfloat16), "dp", scatter_dimension=0, tiled=True
        ).astype(jnp.float32),
        lax.psum_scatter(
            gain_part.astype(jnp.bfloat16), "dp", scatter_dimension=0, tiled=True
        ).astype(jnp.float32),
    )
    return (
        jnp.stack(attended_list),
        jnp.stack(dquery_list),
        grad_rows.reshape(local_seqs, row_count, model_width),
        weight_key,
        weight_value,
        gain_part,
    )


def solution(mesh):
    placed = (P("dp", "ctx", None), P("dp", "ctx", None), P("dp", "ctx", None), P(), P(), P(), P())
    return jax.shard_map(
        body,
        mesh=mesh,
        in_specs=placed,
        out_specs=(
            P("dp", "ctx", None),
            P("dp", "ctx", None),
            P("dp", "ctx", None),
            P(("ctx", "dp"), None),
            P(("ctx", "dp"), None),
            P(("ctx", "dp")),
        ),
        check_vma=False,
    )
```

profile of v0, /device:TPU:0, one launch (start us, length us, event | category | flops | bytes accessed | tf_op | source)
XLA Modules:
  0.0 512.8 jit_solution(5786807104449921285)
XLA Ops:
  7.9 1.5 fusion.8
  10.2 6.5 %copy.154 = bf16[512,4096]{1,0:T(8,128)(2,1)} copy(bf16[512,4096]{0,1:T(8,128)(2,1)} %bitcast.753) | data formatting | bytes 8388608 | tf_op jit(solution)/shard_map/dot_general | solution.py:43
  17.0 3.4 fusion.276
  21.9 3.7 convolution_convert_fusion.1
  27.7 36.9 %all-gather.5.cloned.1.call-done = bf16[2,512,512]{2,1,0:T(8,128)(2,1)} async-done(((bf16[2,64,512]{2,1,0:T(8,128)(2,1)}), bf16[2,512,512]{2,1,0:T(8,128)(2,1)}) %all-gather.5.cloned.1.call-update) | async-done | bytes 1048592 | tf_op jit(solution)/shard_map/all_gather | solution.py:167
  64.6 1.3 slice_bitcast_fusion.2
  65.9 1.7 fusion.264
  68.8 1.7 fusion.94
  70.5 35.8 %all-gather.3.cloned.1.call-done = bf16[2,512,512]{2,1,0:T(8,128)(2,1)} async-done(((bf16[2,64,512]{2,1,0:T(8,128)(2,1)}), bf16[2,512,512]{2,1,0:T(8,128)(2,1)}) %all-gather.3.cloned.1.call-update) | async-done | bytes 1048592 | tf_op jit(solution)/shard_map/all_gather | solution.py:168
  106.3 2.1 slice_bitcast_fusion.3
  108.4 1.4 multiply_reduce_fusion.4
  109.8 2.0 fusion.267
  113.6 2.4 multiply_reduce_fusion.5
  116.8 2.0 fusion.270
  120.6 2.4 multiply_reduce_fusion.6
  123.9 2.4 fusion.273
  126.3 1.2 fusion.119
  127.5 2.4 multiply_reduce_fusion.7
  130.8 2.5 fusion.252
  133.2 1.2 fusion.126
  135.3 1.4 multiply_reduce_fusion
  136.8 2.5 fusion.255
  140.5 1.4 multiply_reduce_fusion.1
  142.8 2.4 fusion.258
  146.4 1.4 multiply_reduce_fusion.2
  148.8 1.9 fusion.261
  150.7 1.2 fusion.123
  152.0 1.5 multiply_reduce_fusion.3
  153.7 1.4 fusion.71
  163.6 2.1 copy.150
  165.8 1.4 fusion.70
  168.1 2.1 copy.137
  172.1 99.3 %all-reduce.7.cloned.1.call-done = (bf16[2,512,512]{2,0,1:T(2,128)(2,1)}, bf16[2,512,512]{2,0,1:T(2,128)(2,1)}) async-done(((bf16[2,512,512]{2,0,1:T(2,128)(2,1)}, bf16[2,512,512]{2,0,1:T(2,128)(2,1)}), (bf16[2,512,512]{2,0,1:T(2,128)(2,1)}, bf16[2,512,512]{2,0,1:T(2,128)(2,1)})) %all-reduce.7.cloned.1.call-update) | async-done | bytes 2097168
  273.4 3.2 convolution_convert_fusion
  277.8 3.3 bitcast_convert_fusion
  283.7 1.8 copy.139
  288.7 1.2 fusion.107
  295.8 68.7 %reduce-scatter.5.cloned.1.call-done = bf16[512,512]{1,0:T(8,128)(2,1)} async-done(((bf16[4096,512]{1,0:T(8,128)(2,1)}), bf16[512,512]{1,0:T(8,128)(2,1)}) %reduce-scatter.5.cloned.1.call-update) | async-done | bytes 524304 | tf_op jit(solution)/shard_map/reduce_scatter | solution.py:213
  364.6 3.8 fusion.277
  368.5 1.7 fusion.18
  370.2 21.3 %all-reduce.2 = bf16[4096]{0:T(1024)(128)(2,1)S(1)} all-reduce(bf16[4096]{0:T(1024)(128)(2,1)S(1)} %get-tuple-element.6), channel_id=8, replica_groups=mesh['ctx'=8,'dp'=4] {'ctx'}, use_global_device_ids=true, to_apply=%region_33.34.clone | all-reduce | flops 4096 | bytes 16384
  391.6 6.0 %all-reduce.3 = bf16[512]{0:T(512)(128)(2,1)S(1)} all-reduce(bf16[512]{0:T(512)(128)(2,1)S(1)} %dynamic-slice.5), channel_id=9, replica_groups=mesh['ctx'=8,'dp'=4] {'dp'}, use_global_device_ids=true, to_apply=%region_34.35.clone | all-reduce | flops 512 | bytes 2048
  397.7 58.8 %reduce-scatter.9.cloned.1.call-done = bf16[512,512]{1,0:T(8,128)(2,1)} async-done(((bf16[4096,512]{1,0:T(8,128)(2,1)}), bf16[512,512]{1,0:T(8,128)(2,1)}) %reduce-scatter.9.cloned.1.call-update) | async-done | bytes 524304 | tf_op jit(solution)/shard_map/reduce_scatter | solution.py:216
  457.1 1.6 fusion.15
  458.7 21.4 %reduce-scatter.7.cloned.1.call-done = bf16[128,512]{1,0:T(8,128)(2,1)} async-done(((bf16[512,512]{1,0:T(8,128)(2,1)}), bf16[128,512]{1,0:T(8,128)(2,1)}) %reduce-scatter.7.cloned.1.call-update) | async-done | bytes 131088 | tf_op jit(solution)/shard_map/reduce_scatter | solution.py:224
  480.1 1.6 convert_element_type.361
  481.7 22.5 %reduce-scatter.11.cloned.1.call-done = bf16[128,512]{1,0:T(8,128)(2,1)} async-done(((bf16[512,512]{1,0:T(8,128)(2,1)}), bf16[128,512]{1,0:T(8,128)(2,1)}) %reduce-scatter.11.cloned.1.call-update) | async-done | bytes 131088 | tf_op jit(solution)/shard_map/reduce_scatter | solution.py:227
  504.3 1.6 convert_element_type.363
  (319 shorter events, 41.8 us)
Async XLA Ops:
  7.2 57.4 %all-gather.5.cloned.1.call-start = ((), (), s32[]{:S(2)}) async-start(), calls=%async_computation.5 | async-start | bytes 1179648 | tf_op jit(solution)/shard_map/all_gather | solution.py:167
  10.2 6.5 %copy-start = (bf16[2,64,4096]{2,1,0:T(8,128)(2,1)S(1)}, bf16[2,64,4096]{2,1,0:T(8,128)(2,1)}, u32[]{:S(2)}) copy-start(bf16[2,64,4096]{2,1,0:T(8,128)(2,1)} %param.7) | copy-start | bytes 3145732
  10.2 6.5 %copy-start.56 = (f32[4096]{0:T(1024)S(1)}, f32[4096]{0:T(1024)}, u32[]{:S(2)}) copy-start(f32[4096]{0:T(1024)} %param.11) | copy-start | bytes 49156
  21.4 84.9 %all-gather.3.cloned.1.call-start = ((), (), s32[]{:S(2)}) async-start(), calls=%async_computation.4 | async-start | bytes 1179648 | tf_op jit(solution)/shard_map/all_gather | solution.py:168
  21.6 4.0 copy-start.80
  21.9 4.0 copy-start.40
  25.6 245.8 %all-reduce.7.cloned.1.call-start = ((), (), s32[]{:S(2)}) async-start(), calls=%async_computation.10 | async-start | bytes 4194304
  26.7 39.2 %copy-start.69 = (bf16[8,4,8,128]{3,2,1,0:T(8,128)(2,1)}, bf16[8,4,8,128]{3,2,1,0:T(8,128)(2,1)S(1)}, u32[]{:S(2)}) copy-start(bf16[8,4,8,128]{3,2,1,0:T(8,128)(2,1)S(1)} %get-tuple-element.83) | copy-start | bytes 196612
  26.8 39.1 %copy-start.79 = (pred[64,512]{1,0:T(8,128)(4,1)}, pred[64,512]{1,0:T(8,128)(4,1)S(1)}, u32[]{:S(2)}) copy-start(pred[64,512]{1,0:T(8,128)(4,1)S(1)} %broadcast_compare_fusion) | copy-start | bytes 98308
  65.8 58.0 %copy-start.4 = (bf16[512,512]{1,0:T(8,128)(2,1)}, bf16[512,512]{1,0:T(8,128)(2,1)S(1)}, u32[]{:S(2)}) copy-start(bf16[512,512]{1,0:T(8,128)(2,1)S(1)} %get-tuple-element.14) | copy-start | bytes 1572868
  65.8 82.9 %copy-start.2 = (bf16[512,512]{1,0:T(8,128)(2,1)}, bf16[512,512]{1,0:T(8,128)(2,1)S(1)}, u32[]{:S(2)}) copy-start(bf16[512,512]{1,0:T(8,128)(2,1)S(1)} %get-tuple-element.15) | copy-start | bytes 1572868
  109.8 6.2 %copy-start.31 = (bf16[8,4,8,128]{3,2,1,0:T(8,128)(2,1)S(1)}, bf16[8,4,8,128]{3,2,1,0:T(8,128)(2,1)}, u32[]{:S(2)}) copy-start(bf16[8,4,8,128]{3,2,1,0:T(8,128)(2,1)} %get-tuple-element.78) | copy-start | bytes 196612
  111.8 8.8 %copy-start.29 = (bf16[8,4,8,128]{3,2,1,0:T(8,128)(2,1)S(1)}, bf16[8,4,8,128]{3,2,1,0:T(8,128)(2,1)}, u32[]{:S(2)}) copy-start(bf16[8,4,8,128]{3,2,1,0:T(8,128)(2,1)} %get-tuple-element.77) | copy-start | bytes 196612
  113.5 10.3 %copy-start.65 = (bf16[8,4,8,128]{3,2,1,0:T(8,128)(2,1)S(1)}, bf16[8,4,8,128]{3,2,1,0:T(8,128)(2,1)}, u32[]{:S(2)}) copy-start(bf16[8,4,8,128]{3,2,1,0:T(8,128)(2,1)} %get-tuple-element.84) | copy-start | bytes 196612
  118.8 8.7 %copy-start.27 = (bf16[8,4,8,128]{3,2,1,0:T(8,128)(2,1)S(1)}, bf16[8,4,8,128]{3,2,1,0:T(8,128)(2,1)}, u32[]{:S(2)}) copy-start(bf16[8,4,8,128]{3,2,1,0:T(8,128)(2,1)} %get-tuple-element.80) | copy-start | bytes 196612
  120.5 10.2 %copy-start.63 = (bf16[8,4,8,128]{3,2,1,0:T(8,128)(2,1)S(1)}, bf16[8,4,8,128]{3,2,1,0:T(8,128)(2,1)}, u32[]{:S(2)}) copy-start(bf16[8,4,8,128]{3,2,1,0:T(8,128)(2,1)} %get-tuple-element.37) | copy-start | bytes 196612
  126.3 8.1 %copy-start.25 = (bf16[8,4,8,128]{3,2,1,0:T(8,128)(2,1)S(1)}, bf16[8,4,8,128]{3,2,1,0:T(8,128)(2,1)}, u32[]{:S(2)}) copy-start(bf16[8,4,8,128]{3,2,1,0:T(8,128)(2,1)} %get-tuple-element.29) | copy-start | bytes 196612
  126.3 9.1 %copy-start.6 = (bf16[512,512]{1,0:T(8,128)(2,1)S(1)}, bf16[512,512]{1,0:T(8,128)(2,1)}, u32[]{:S(2)}) copy-start(bf16[512,512]{1,0:T(8,128)(2,1)} %get-tuple-element.13) | copy-start | bytes 1572868
  127.5 9.3 %copy-start.61 = (bf16[8,4,8,128]{3,2,1,0:T(8,128)(2,1)S(1)}, bf16[8,4,8,128]{3,2,1,0:T(8,128)(2,1)}, u32[]{:S(2)}) copy-start(bf16[8,4,8,128]{3,2,1,0:T(8,128)(2,1)} %get-tuple-element.38) | copy-start | bytes 196612
  133.2 7.2 %copy-start.23 = (bf16[8,4,8,128]{3,2,1,0:T(8,128)(2,1)S(1)}, bf16[8,4,8,128]{3,2,1,0:T(8,128)(2,1)}, u32[]{:S(2)}) copy-start(bf16[8,4,8,128]{3,2,1,0:T(8,128)(2,1)} %get-tuple-element.30) | copy-start | bytes 196612
  134.4 8.4 %copy-start.59 = (bf16[8,4,8,128]{3,2,1,0:T(8,128)(2,1)S(1)}, bf16[8,4,8,128]{3,2,1,0:T(8,128)(2,1)}, u32[]{:S(2)}) copy-start(bf16[8,4,8,128]{3,2,1,0:T(8,128)(2,1)} %get-tuple-element.39) | copy-start | bytes 196612
  139.3 7.2 %copy-start.21 = (bf16[8,4,8,128]{3,2,1,0:T(8,128)(2,1)S(1)}, bf16[8,4,8,128]{3,2,1,0:T(8,128)(2,1)}, u32[]{:S(2)}) copy-start(bf16[8,4,8,128]{3,2,1,0:T(8,128)(2,1)} %get-tuple-element.31) | copy-start | bytes 196612
  140.4 8.3 %copy-start.57 = (bf16[8,4,8,128]{3,2,1,0:T(8,128)(2,1)S(1)}, bf16[8,4,8,128]{3,2,1,0:T(8,128)(2,1)}, u32[]{:S(2)}) copy-start(bf16[8,4,8,128]{3,2,1,0:T(8,128)(2,1)} %get-tuple-element.36) | copy-start | bytes 196612
  145.2 6.7 %copy-start.20 = (bf16[8,4,8,128]{3,2,1,0:T(8,128)(2,1)S(1)}, bf16[8,4,8,128]{3,2,1,0:T(8,128)(2,1)}, u32[]{:S(2)}) copy-start(bf16[8,4,8,128]{3,2,1,0:T(8,128)(2,1)} %get-tuple-element.28) | copy-start | bytes 196612
  150.7 4.4 copy-start.70
  150.7 5.3 %copy-start.8 = (bf16[512,512]{1,0:T(8,128)(2,1)S(1)}, bf16[512,512]{1,0:T(8,128)(2,1)}, u32[]{:S(2)}) copy-start(bf16[512,512]{1,0:T(8,128)(2,1)} %copy-done.7) | copy-start | bytes 1572868
  150.7 5.3 %copy-start.32 = (bf16[8,4,8,128]{3,2,1,0:T(8,128)(2,1)S(1)}, bf16[8,4,8,128]{3,2,1,0:T(8,128)(2,1)}, u32[]{:S(2)}) copy-start(bf16[8,4,8,128]{3,2,1,0:T(8,128)(2,1)} %get-tuple-element.78) | copy-start | bytes 196612
  150.7 5.3 %copy-start.34 = (f32[4,64,512]{2,1,0:T(8,128)S(1)}, f32[4,64,512]{2,1,0:T(8,128)}, u32[]{:S(2)}) copy-start(f32[4,64,512]{2,1,0:T(8,128)} %get-tuple-element.55) | copy-start | bytes 1572868
  150.7 5.3 %copy-start.84 = (f32[4,64]{1,0:T(4,128)S(1)}, f32[4,64]{1,0:T(4,128)}, u32[]{:S(2)}) copy-start(f32[4,64]{1,0:T(4,128)} %copy-done.83) | copy-start | bytes 3076
  150.7 5.3 %copy-start.85 = (f32[64,4]{0,1:T(4,128)S(1)}, f32[64,4]{0,1:T(4,128)}, u32[]{:S(2)}) copy-start(f32[64,4]{0,1:T(4,128)} %get-tuple-element.70) | copy-start | bytes 3076
  170.2 194.3 %reduce-scatter.5.cloned.1.call-start = ((), (), s32[]{:S(2)}) async-start(), calls=%async_computation.6 | async-start | bytes 4718592 | tf_op jit(solution)/shard_map/reduce_scatter | solution.py:213
  276.7 179.8 %reduce-scatter.9.cloned.1.call-start = ((), (), s32[]{:S(2)}) async-start(), calls=%async_computation.8 | async-start | bytes 4718592 | tf_op jit(solution)/shard_map/reduce_scatter | solution.py:216
  281.1 5.0 copy-start.81
  281.1 5.6 %copy-start.5 = (bf16[512,512]{1,0:T(8,128)(2,1)S(1)}, bf16[512,512]{1,0:T(8,128)(2,1)}, u32[]{:S(2)}) copy-start(bf16[512,512]{1,0:T(8,128)(2,1)} %copy-done.4) | copy-start | bytes 1572868
  281.1 5.8 %copy-start.10 = (bf16[4,64,512]{2,1,0:T(8,128)(2,1)S(1)}, bf16[4,64,512]{2,1,0:T(8,128)(2,1)}, u32[]{:S(2)}) copy-start(bf16[4,64,512]{2,1,0:T(8,128)(2,1)} %copy-done.9) | copy-start | bytes 786436
  281.1 6.1 %copy-start.12 = (bf16[4,64,512]{2,1,0:T(8,128)(2,1)S(1)}, bf16[4,64,512]{2,1,0:T(8,128)(2,1)}, u32[]{:S(2)}) copy-start(bf16[4,64,512]{2,1,0:T(8,128)(2,1)} %copy-done.11) | copy-start | bytes 786436
  281.1 7.6 %copy-start.3 = (bf16[512,512]{1,0:T(8,128)(2,1)S(1)}, bf16[512,512]{1,0:T(8,128)(2,1)}, u32[]{:S(2)}) copy-start(bf16[512,512]{1,0:T(8,128)(2,1)} %copy-done.2) | copy-start | bytes 1572868
  281.1 199.0 %reduce-scatter.7.cloned.1.call-start = ((), (), s32[]{:S(2)}) async-start(), calls=%async_computation.7 | async-start | bytes 655360 | tf_op jit(solution)/shard_map/reduce_scatter | solution.py:224
  286.9 6.6 %copy-start.71 = (bf16[128,4,64]{0,2,1:T(8,128)(2,1)S(1)}, bf16[128,4,64]{0,2,1:T(8,128)(2,1)}, u32[]{:S(2)}) copy-start(bf16[128,4,64]{0,2,1:T(8,128)(2,1)} %get-tuple-element.69) | copy-start | bytes 196612
  286.9 6.7 %copy-start.72 = (bf16[128,4,64]{0,2,1:T(8,128)(2,1)S(1)}, bf16[128,4,64]{0,2,1:T(8,128)(2,1)}, u32[]{:S(2)}) copy-start(bf16[128,4,64]{0,2,1:T(8,128)(2,1)} %get-tuple-element.71) | copy-start | bytes 196612
  286.9 6.7 %copy-start.73 = (bf16[128,4,64]{0,2,1:T(8,128)(2,1)S(1)}, bf16[128,4,64]{0,2,1:T(8,128)(2,1)}, u32[]{:S(2)}) copy-start(bf16[128,4,64]{0,2,1:T(8,128)(2,1)} %get-tuple-element.73) | copy-start | bytes 196612
  287.2 6.5 %copy-start.74 = (bf16[128,4,64]{0,2,1:T(8,128)(2,1)S(1)}, bf16[128,4,64]{0,2,1:T(8,128)(2,1)}, u32[]{:S(2)}) copy-start(bf16[128,4,64]{0,2,1:T(8,128)(2,1)} %get-tuple-element.75) | copy-start | bytes 196612
  287.2 6.5 %copy-start.75 = (bf16[128,4,64]{0,2,1:T(8,128)(2,1)S(1)}, bf16[128,4,64]{0,2,1:T(8,128)(2,1)}, u32[]{:S(2)}) copy-start(bf16[128,4,64]{0,2,1:T(8,128)(2,1)} %get-tuple-element.61) | copy-start | bytes 196612
  287.2 6.5 %copy-start.76 = (bf16[128,4,64]{0,2,1:T(8,128)(2,1)S(1)}, bf16[128,4,64]{0,2,1:T(8,128)(2,1)}, u32[]{:S(2)}) copy-start(bf16[128,4,64]{0,2,1:T(8,128)(2,1)} %get-tuple-element.63) | copy-start | bytes 196612
  287.2 6.5 %copy-start.77 = (bf16[128,4,64]{0,2,1:T(8,128)(2,1)S(1)}, bf16[128,4,64]{0,2,1:T(8,128)(2,1)}, u32[]{:S(2)}) copy-start(bf16[128,4,64]{0,2,1:T(8,128)(2,1)} %get-tuple-element.65) | copy-start | bytes 196612
  287.5 6.3 %copy-start.78 = (bf16[128,4,64]{0,2,1:T(8,128)(2,1)S(1)}, bf16[128,4,64]{0,2,1:T(8,128)(2,1)}, u32[]{:S(2)}) copy-start(bf16[128,4,64]{0,2,1:T(8,128)(2,1)} %get-tuple-element.67) | copy-start | bytes 196612
  364.6 139.7 %reduce-scatter.11.cloned.1.call-start = ((), (), s32[]{:S(2)}) async-start(), calls=%async_computation.9 | async-start | bytes 655360 | tf_op jit(solution)/shard_map/reduce_scatter | solution.py:227
  368.5 88.6 %copy-start.98 = (f32[128]{0:T(128)S(1)}, f32[128]{0:T(128)}, u32[]{:S(2)}) copy-start(f32[128]{0:T(128)} %multiply_multiply_fusion) | copy-start | bytes 1540
  (60 other events, 118.6 us)
Sparse Core Ops, SparseCore 0:
  21.6 42.9 all-gather.4
  67.3 38.9 all-gather.2
  170.3 101.0 all-reduce.6
  276.8 87.6 reduce-scatter.4
  368.0 88.4 reduce-scatter.8
  458.8 21.2 reduce-scatter.6
  482.6 21.6 reduce-scatter.10
where the time goes:
time: 514 us; the launch traced here: 513 us
  waiting for transfers between devices  344 us (67%)
  matrix products  75.4 us (15%)
  blocking collectives  27.4 us (5%)
  local copies, waits for them, and re-layouts  26.2 us (5%)
  other arithmetic  21.8 us (4%)
  between operations  17.6 us (3%)
    unnamed x8, waiting for transfers between devices  99.4 us
    reduce_scatter x1, waiting for transfers between devices, body(): lax.psum_scatter(weight_key.astype(jnp.bfloat16), 'ctx', scatter_dimensio...  68.7 us
    reduce_scatter x1, waiting for transfers between devices, body(): lax.psum_scatter(weight_value.astype(jnp.bfloat16), 'ctx', scatter_dimens...  58.8 us
    all_gather x1, waiting for transfers between devices, body(): lax.all_gather(rotated_keys, 'ctx', axis=1, tiled=True)  36.9 us
    all_gather x1, waiting for transfers between devices, body(): lax.all_gather(value_rows, 'ctx', axis=1, tiled=True)  35.8 us
    unnamed x2, blocking collectives  27.4 us
    reduce_scatter x1, waiting for transfers between devices, body(): lax.psum_scatter(weight_value.astype(jnp.bfloat16), 'dp', scatter_dimensi...  22.5 us
    reduce_scatter x1, waiting for transfers between devices, body(): lax.psum_scatter(weight_key.astype(jnp.bfloat16), 'dp', scatter_dimension...  21.4 us
  transfers between devices with their start and end apart: 7, of which 7 were waited for; matrix products, arithmetic and copies ran while one was open for 8% of the time, Pallas kernels for 0%

commit v1 on v0

--- a/solution.py
+++ b/solution.py
@@ -165,7 +165,7 @@
     value_rows = value_rows.reshape(local_seqs, row_count, kv_width)
     all_keys, all_values = (
         lax.all_gather(rotated_keys, "ctx", axis=1, tiled=True),
-        lax.all_gather(value_rows, "ctx", axis=1, tiled=True),
+        jnp.concatenate(lax.all_gather(value_rows, "ctx"), axis=1),
     )
     attended_list, dquery_list, key_list, value_list = ([], [], [], [])
     for sequence in range(local_seqs):

time: 514 us -> 516 us (level)
  waiting for transfers between devices: 344 us -> 334 us
  matrix products: 75.4 us -> 81.1 us
    all_gather x1, waiting for transfers between devices: 35.8 us -> 27.2 us  [body(): lax.all_gather(value_rows, 'ctx')]
  transfers between devices with their start and end apart: 7 -> 7, of which waited for: 7 -> 7; matrix products, arithmetic and copies ran while one was open for 8% -> 9% of each run, Pallas kernels for 0% -> 0%
where the time goes in v1:
time: 516 us; the launch traced here: 514 us
  waiting for transfers between devices  334 us (65%)
  matrix products  81.1 us (16%)
  blocking collectives  27.7 us (5%)
  local copies, waits for them, and re-layouts  26.6 us (5%)
  other arithmetic  25.7 us (5%)
  between operations  17.6 us (3%)
    unnamed x8, waiting for transfers between devices  99.5 us
    reduce_scatter x1, waiting for transfers between devices, body(): lax.psum_scatter(weight_key.astype(jnp.bfloat16), 'ctx', scatter_dimensio...  68.6 us
    reduce_scatter x1, waiting for transfers between devices, body(): lax.psum_scatter(weight_value.astype(jnp.bfloat16), 'ctx', scatter_dimens...  57.3 us
    all_gather x1, waiting for transfers between devices, body(): lax.all_gather(rotated_keys, 'ctx', axis=1, tiled=True)  39.5 us
    unnamed x2, blocking collectives  27.7 us
    all_gather x1, waiting for transfers between devices, body(): lax.all_gather(value_rows, 'ctx')  27.2 us
    reduce_scatter x1, waiting for transfers between devices, body(): lax.psum_scatter(weight_value.astype(jnp.bfloat16), 'dp', scatter_dimensi...  22.5 us
    reduce_scatter x1, waiting for transfers between devices, body(): lax.psum_scatter(weight_key.astype(jnp.bfloat16), 'dp', scatter_dimension...  19.9 us
  transfers between devices with their start and end apart: 7, of which 7 were waited for; matrix products, arithmetic and copies ran while one was open for 9% of the time, Pallas kernels for 0%

profile of v1, /device:TPU:0, one launch (start us, length us, event | category | flops | bytes accessed | tf_op | source)
XLA Modules:
  0.0 513.9 jit_solution(16306066705791413198)
XLA Ops:
  7.2 1.5 fusion.8
  8.8 1.6 fusion.12
  10.4 3.6 convolution_convert_fusion.1
  15.4 6.5 %copy.154 = bf16[512,4096]{1,0:T(8,128)(2,1)} copy(bf16[512,4096]{0,1:T(8,128)(2,1)} %bitcast.752) | data formatting | bytes 8388608 | tf_op jit(solution)/shard_map/dot_general | solution.py:43
  22.2 3.5 fusion.277
  26.9 1.4 broadcast_compare_fusion
  30.0 27.2 %all-gather.3.cloned.1.call-done = bf16[8,2,64,512]{3,2,1,0:T(8,128)(2,1)} async-done(((bf16[1,2,64,512]{3,2,1,0:T(8,128)(2,1)}), bf16[8,2,64,512]{3,2,1,0:T(8,128)(2,1)}) %all-gather.3.cloned.1.call-update) | async-done | bytes 1048592 | tf_op jit(solution)/shard_map/all_gather | solution.py:168
  57.2 2.3 fusion.251
  59.4 39.5 %all-gather.5.cloned.1.call-done = bf16[2,512,512]{2,1,0:T(8,128)(2,1)} async-done(((bf16[2,64,512]{2,1,0:T(8,128)(2,1)}), bf16[2,512,512]{2,1,0:T(8,128)(2,1)}) %all-gather.5.cloned.1.call-update) | async-done | bytes 1048592 | tf_op jit(solution)/shard_map/all_gather | solution.py:167
  100.2 2.6 fusion.265
  104.0 1.7 fusion.94
  105.7 2.4 multiply_reduce_fusion.4
  108.1 2.5 fusion.268
  111.7 2.3 multiply_reduce_fusion.5
  114.0 1.7 fusion.93
  115.8 2.5 fusion.271
  119.4 2.3 multiply_reduce_fusion.6
  121.8 1.7 fusion.92
  123.5 2.5 fusion.274
  127.2 2.3 multiply_reduce_fusion.7
  129.6 1.7 fusion.91
  131.3 2.5 fusion.253
  135.9 1.4 multiply_reduce_fusion
  137.3 2.0 fusion.256
  141.1 1.5 multiply_reduce_fusion.1
  143.4 1.9 fusion.259
  146.5 1.4 multiply_reduce_fusion.2
  148.9 1.9 fusion.262
  152.0 1.5 multiply_reduce_fusion.3
  153.7 1.4 fusion.71
  164.3 2.1 copy.150
  166.5 1.4 fusion.70
  169.1 2.1 copy.137
  173.1 99.4 %all-reduce.7.cloned.1.call-done = (bf16[2,512,512]{2,0,1:T(2,128)(2,1)}, bf16[2,512,512]{2,0,1:T(2,128)(2,1)}) async-done(((bf16[2,512,512]{2,0,1:T(2,128)(2,1)}, bf16[2,512,512]{2,0,1:T(2,128)(2,1)}), (bf16[2,512,512]{2,0,1:T(2,128)(2,1)}, bf16[2,512,512]{2,0,1:T(2,128)(2,1)})) %all-reduce.7.cloned.1.call-update) | async-done | bytes 2097168
  274.5 3.3 convolution_convert_fusion
  278.9 3.3 bitcast_convert_fusion
  284.8 1.8 copy.139
  297.0 68.6 %reduce-scatter.5.cloned.1.call-done = bf16[512,512]{1,0:T(8,128)(2,1)} async-done(((bf16[4096,512]{1,0:T(8,128)(2,1)}), bf16[512,512]{1,0:T(8,128)(2,1)}) %reduce-scatter.5.cloned.1.call-update) | async-done | bytes 524304 | tf_op jit(solution)/shard_map/reduce_scatter | solution.py:213
  365.7 3.8 fusion.278
  369.5 3.0 fusion.18
  372.5 21.7 %all-reduce.2 = bf16[4096]{0:T(1024)(128)(2,1)S(1)} all-reduce(bf16[4096]{0:T(1024)(128)(2,1)S(1)} %get-tuple-element.6), channel_id=8, replica_groups=mesh['ctx'=8,'dp'=4] {'ctx'}, use_global_device_ids=true, to_apply=%region_33.34.clone | all-reduce | flops 4096 | bytes 16384
  394.3 6.0 %all-reduce.3 = bf16[512]{0:T(512)(128)(2,1)S(1)} all-reduce(bf16[512]{0:T(512)(128)(2,1)S(1)} %dynamic-slice.5), channel_id=9, replica_groups=mesh['ctx'=8,'dp'=4] {'dp'}, use_global_device_ids=true, to_apply=%region_34.35.clone | all-reduce | flops 512 | bytes 2048
  400.4 57.3 %reduce-scatter.9.cloned.1.call-done = bf16[512,512]{1,0:T(8,128)(2,1)} async-done(((bf16[4096,512]{1,0:T(8,128)(2,1)}), bf16[512,512]{1,0:T(8,128)(2,1)}) %reduce-scatter.9.cloned.1.call-update) | async-done | bytes 524304 | tf_op jit(solution)/shard_map/reduce_scatter | solution.py:216
  458.2 3.2 fusion.15
  461.4 19.9 %reduce-scatter.7.cloned.1.call-done = bf16[128,512]{1,0:T(8,128)(2,1)} async-done(((bf16[512,512]{1,0:T(8,128)(2,1)}), bf16[128,512]{1,0:T(8,128)(2,1)}) %reduce-scatter.7.cloned.1.call-update) | async-done | bytes 131088 | tf_op jit(solution)/shard_map/reduce_scatter | solution.py:224
  481.3 1.6 convert_element_type.361
  482.9 22.5 %reduce-scatter.11.cloned.1.call-done = bf16[128,512]{1,0:T(8,128)(2,1)} async-done(((bf16[512,512]{1,0:T(8,128)(2,1)}), bf16[128,512]{1,0:T(8,128)(2,1)}) %reduce-scatter.11.cloned.1.call-update) | async-done | bytes 131088 | tf_op jit(solution)/shard_map/reduce_scatter | solution.py:227
  505.5 1.6 convert_element_type.363
  (301 shorter events, 44.9 us)
Async XLA Ops:
  7.2 50.0 %all-gather.3.cloned.1.call-start = ((), (), s32[]{:S(2)}) async-start(), calls=%async_computation.4 | async-start | bytes 1179648 | tf_op jit(solution)/shard_map/all_gather | solution.py:168
  8.8 5.1 %copy-start.70 = (f32[128]{0:T(128)}, f32[128]{0:T(128)S(1)}, u32[]{:S(2)}) copy-start(f32[128]{0:T(128)S(1)} %rsqrt.16) | copy-start | bytes 1540
  10.4 3.7 copy-start.89
  14.0 84.9 %all-gather.5.cloned.1.call-start = ((), (), s32[]{:S(2)}) async-start(), calls=%async_computation.5 | async-start | bytes 1179648 | tf_op jit(solution)/shard_map/all_gather | solution.py:167
  15.3 6.5 %copy-start = (bf16[2,64,4096]{2,1,0:T(8,128)(2,1)S(1)}, bf16[2,64,4096]{2,1,0:T(8,128)(2,1)}, u32[]{:S(2)}) copy-start(bf16[2,64,4096]{2,1,0:T(8,128)(2,1)} %param.7) | copy-start | bytes 3145732
  15.4 6.5 %copy-start.51 = (f32[4096]{0:T(1024)S(1)}, f32[4096]{0:T(1024)}, u32[]{:S(2)}) copy-start(f32[4096]{0:T(1024)} %param.11) | copy-start | bytes 49156
  25.7 3.5 copy-start.36
  26.7 245.8 %all-reduce.7.cloned.1.call-start = ((), (), s32[]{:S(2)}) async-start(), calls=%async_computation.10 | async-start | bytes 4194304
  29.9 105.9 %copy-start.24 = (bf16[8,4,8,128]{3,2,1,0:T(8,128)(2,1)}, bf16[8,4,8,128]{3,2,1,0:T(8,128)(2,1)S(1)}, u32[]{:S(2)}) copy-start(bf16[8,4,8,128]{3,2,1,0:T(8,128)(2,1)S(1)} %get-tuple-element.29) | copy-start | bytes 196612
  29.9 112.6 %copy-start.22 = (bf16[8,4,8,128]{3,2,1,0:T(8,128)(2,1)}, bf16[8,4,8,128]{3,2,1,0:T(8,128)(2,1)S(1)}, u32[]{:S(2)}) copy-start(bf16[8,4,8,128]{3,2,1,0:T(8,128)(2,1)S(1)} %get-tuple-element.30) | copy-start | bytes 196612
  29.9 118.0 %copy-start.20 = (bf16[8,4,8,128]{3,2,1,0:T(8,128)(2,1)}, bf16[8,4,8,128]{3,2,1,0:T(8,128)(2,1)S(1)}, u32[]{:S(2)}) copy-start(bf16[8,4,8,128]{3,2,1,0:T(8,128)(2,1)S(1)} %get-tuple-element.31) | copy-start | bytes 196612
  29.9 123.5 %copy-start.19 = (bf16[8,4,8,128]{3,2,1,0:T(8,128)(2,1)}, bf16[8,4,8,128]{3,2,1,0:T(8,128)(2,1)S(1)}, u32[]{:S(2)}) copy-start(bf16[8,4,8,128]{3,2,1,0:T(8,128)(2,1)S(1)} %get-tuple-element.28) | copy-start | bytes 196612
  100.2 23.3 %copy-start.4 = (bf16[512,512]{1,0:T(8,128)(2,1)}, bf16[512,512]{1,0:T(8,128)(2,1)S(1)}, u32[]{:S(2)}) copy-start(bf16[512,512]{1,0:T(8,128)(2,1)S(1)} %get-tuple-element.14) | copy-start | bytes 1572868
  100.2 48.6 %copy-start.2 = (bf16[512,512]{1,0:T(8,128)(2,1)}, bf16[512,512]{1,0:T(8,128)(2,1)S(1)}, u32[]{:S(2)}) copy-start(bf16[512,512]{1,0:T(8,128)(2,1)S(1)} %get-tuple-element.15) | copy-start | bytes 1572868
  126.0 9.9 %copy-start.6 = (bf16[1,8,64,512]{3,2,0,1:T(8,128)(2,1)S(1)}, bf16[1,8,64,512]{3,2,0,1:T(8,128)(2,1)}, u32[]{:S(2)}) copy-start(bf16[1,8,64,512]{3,2,0,1:T(8,128)(2,1)} %get-tuple-element.13) | copy-start | bytes 1572868
  141.0 7.8 %copy-start.52 = (bf16[8,4,8,128]{3,2,1,0:T(8,128)(2,1)S(1)}, bf16[8,4,8,128]{3,2,1,0:T(8,128)(2,1)}, u32[]{:S(2)}) copy-start(bf16[8,4,8,128]{3,2,1,0:T(8,128)(2,1)} %get-tuple-element.36) | copy-start | bytes 196612
  145.4 8.1 %copy-start.85 = (f32[4,64]{1,0:T(4,128)}, f32[4,64]{1,0:T(4,128)S(1)}, u32[]{:S(2)}) copy-start(f32[4,64]{1,0:T(4,128)S(1)} %get-tuple-element.48) | copy-start | bytes 3076
  150.7 3.0 copy-start.76
  150.7 4.4 copy-start.60
  150.7 5.3 %copy-start.7 = (bf16[1,8,64,512]{3,2,0,1:T(8,128)(2,1)S(1)}, bf16[1,8,64,512]{3,2,0,1:T(8,128)(2,1)}, u32[]{:S(2)}) copy-start(bf16[1,8,64,512]{3,2,0,1:T(8,128)(2,1)} %get-tuple-element.12) | copy-start | bytes 1572868
  150.7 5.3 %copy-start.28 = (bf16[8,4,8,128]{3,2,1,0:T(8,128)(2,1)S(1)}, bf16[8,4,8,128]{3,2,1,0:T(8,128)(2,1)}, u32[]{:S(2)}) copy-start(bf16[8,4,8,128]{3,2,1,0:T(8,128)(2,1)} %get-tuple-element.78) | copy-start | bytes 196612
  150.7 5.3 %copy-start.29 = (f32[4,64,512]{2,1,0:T(8,128)S(1)}, f32[4,64,512]{2,1,0:T(8,128)}, u32[]{:S(2)}) copy-start(f32[4,64,512]{2,1,0:T(8,128)} %get-tuple-element.55) | copy-start | bytes 1572868
  150.7 5.3 %copy-start.73 = (f32[4,64]{1,0:T(4,128)S(1)}, f32[4,64]{1,0:T(4,128)}, u32[]{:S(2)}) copy-start(f32[4,64]{1,0:T(4,128)} %get-tuple-element.54) | copy-start | bytes 3076
  150.8 5.3 %copy-start.74 = (f32[64,4]{0,1:T(4,128)S(1)}, f32[64,4]{0,1:T(4,128)}, u32[]{:S(2)}) copy-start(f32[64,4]{0,1:T(4,128)} %get-tuple-element.70) | copy-start | bytes 3076
  161.3 2.8 copy-start.37
  161.3 2.8 copy-start.41
  161.3 2.8 copy-start.42
  161.3 2.8 copy-start.43
  171.2 194.4 %reduce-scatter.5.cloned.1.call-start = ((), (), s32[]{:S(2)}) async-start(), calls=%async_computation.6 | async-start | bytes 4718592 | tf_op jit(solution)/shard_map/reduce_scatter | solution.py:213
  277.9 179.8 %reduce-scatter.9.cloned.1.call-start = ((), (), s32[]{:S(2)}) async-start(), calls=%async_computation.8 | async-start | bytes 4718592 | tf_op jit(solution)/shard_map/reduce_scatter | solution.py:216
  282.2 5.0 copy-start.71
  282.2 5.6 %copy-start.5 = (bf16[512,512]{1,0:T(8,128)(2,1)S(1)}, bf16[512,512]{1,0:T(8,128)(2,1)}, u32[]{:S(2)}) copy-start(bf16[512,512]{1,0:T(8,128)(2,1)} %copy-done.4) | copy-start | bytes 1572868
  282.2 5.9 %copy-start.9 = (bf16[4,64,512]{2,1,0:T(8,128)(2,1)S(1)}, bf16[4,64,512]{2,1,0:T(8,128)(2,1)}, u32[]{:S(2)}) copy-start(bf16[4,64,512]{2,1,0:T(8,128)(2,1)} %copy-done.8) | copy-start | bytes 786436
  282.2 6.2 %copy-start.11 = (bf16[4,64,512]{2,1,0:T(8,128)(2,1)S(1)}, bf16[4,64,512]{2,1,0:T(8,128)(2,1)}, u32[]{:S(2)}) copy-start(bf16[4,64,512]{2,1,0:T(8,128)(2,1)} %copy-done.10) | copy-start | bytes 786436
  282.2 7.7 %copy-start.3 = (bf16[512,512]{1,0:T(8,128)(2,1)S(1)}, bf16[512,512]{1,0:T(8,128)(2,1)}, u32[]{:S(2)}) copy-start(bf16[512,512]{1,0:T(8,128)(2,1)} %copy-done.2) | copy-start | bytes 1572868
  282.2 199.1 %reduce-scatter.7.cloned.1.call-start = ((), (), s32[]{:S(2)}) async-start(), calls=%async_computation.7 | async-start | bytes 655360 | tf_op jit(solution)/shard_map/reduce_scatter | solution.py:224
  288.1 6.7 %copy-start.61 = (bf16[128,4,64]{0,2,1:T(8,128)(2,1)S(1)}, bf16[128,4,64]{0,2,1:T(8,128)(2,1)}, u32[]{:S(2)}) copy-start(bf16[128,4,64]{0,2,1:T(8,128)(2,1)} %get-tuple-element.69) | copy-start | bytes 196612
  288.1 6.7 %copy-start.62 = (bf16[128,4,64]{0,2,1:T(8,128)(2,1)S(1)}, bf16[128,4,64]{0,2,1:T(8,128)(2,1)}, u32[]{:S(2)}) copy-start(bf16[128,4,64]{0,2,1:T(8,128)(2,1)} %get-tuple-element.71) | copy-start | bytes 196612
  288.1 6.7 %copy-start.63 = (bf16[128,4,64]{0,2,1:T(8,128)(2,1)S(1)}, bf16[128,4,64]{0,2,1:T(8,128)(2,1)}, u32[]{:S(2)}) copy-start(bf16[128,4,64]{0,2,1:T(8,128)(2,1)} %get-tuple-element.73) | copy-start | bytes 196612
  288.3 6.5 %copy-start.64 = (bf16[128,4,64]{0,2,1:T(8,128)(2,1)S(1)}, bf16[128,4,64]{0,2,1:T(8,128)(2,1)}, u32[]{:S(2)}) copy-start(bf16[128,4,64]{0,2,1:T(8,128)(2,1)} %get-tuple-element.75) | copy-start | bytes 196612
  288.3 6.5 %copy-start.65 = (bf16[128,4,64]{0,2,1:T(8,128)(2,1)S(1)}, bf16[128,4,64]{0,2,1:T(8,128)(2,1)}, u32[]{:S(2)}) copy-start(bf16[128,4,64]{0,2,1:T(8,128)(2,1)} %get-tuple-element.61) | copy-start | bytes 196612
  288.4 6.5 %copy-start.66 = (bf16[128,4,64]{0,2,1:T(8,128)(2,1)S(1)}, bf16[128,4,64]{0,2,1:T(8,128)(2,1)}, u32[]{:S(2)}) copy-start(bf16[128,4,64]{0,2,1:T(8,128)(2,1)} %get-tuple-element.63) | copy-start | bytes 196612
  288.4 6.5 %copy-start.67 = (bf16[128,4,64]{0,2,1:T(8,128)(2,1)S(1)}, bf16[128,4,64]{0,2,1:T(8,128)(2,1)}, u32[]{:S(2)}) copy-start(bf16[128,4,64]{0,2,1:T(8,128)(2,1)} %get-tuple-element.65) | copy-start | bytes 196612
  288.6 6.3 %copy-start.68 = (bf16[128,4,64]{0,2,1:T(8,128)(2,1)S(1)}, bf16[128,4,64]{0,2,1:T(8,128)(2,1)}, u32[]{:S(2)}) copy-start(bf16[128,4,64]{0,2,1:T(8,128)(2,1)} %get-tuple-element.67) | copy-start | bytes 196612
  365.6 3.9 copy-start.72
  365.6 139.8 %reduce-scatter.11.cloned.1.call-start = ((), (), s32[]{:S(2)}) async-start(), calls=%async_computation.9 | async-start | bytes 655360 | tf_op jit(solution)/shard_map/reduce_scatter | solution.py:227
  365.7 3.8 copy-start.1
  369.5 88.7 %copy-start.88 = (f32[128]{0:T(128)S(1)}, f32[128]{0:T(128)}, u32[]{:S(2)}) copy-start(f32[128]{0:T(128)} %multiply_multiply_fusion) | copy-start | bytes 1540
  (51 other events, 102.8 us)
Sparse Core Ops, SparseCore 0:
  14.1 42.9 all-gather.2
  59.9 38.9 all-gather.4
  171.3 101.0 all-reduce.6
  278.0 87.5 reduce-scatter.4
  369.1 88.5 reduce-scatter.8
  460.0 21.2 reduce-scatter.6
  483.8 21.6 reduce-scatter.10
